TPU v7x, 32 devices: a whole 2x2x4 slice. The times are simulated.
32 devices in a mesh: grp: 2 (over x), rep: 8 (over z, y), blk: 2 (over core).
Axes of the slice: x: 2, y: 2, z: 4, core: 2. Of those that a mesh axis runs over, the one named last changes fastest.
Arguments:
- factors: float32 [16, 1280, 1280], P('grp', ('blk', 'rep')), as said below
- damping: float32 [16], P('grp'), may hold values from 0.1 to 1
Outputs:
- root: float32 [16, 1280, 1280], P('grp', ('blk', 'rep'))
- inv_root: float32 [16, 1280, 1280], P('grp', ('blk', 'rep'))
Inputs may be any that keep to these rules, and one draw needn't show every extreme that they name: `factors`: every factor is symmetric positive semidefinite.
All inputs are finite; a program needn't handle non-finite values.
Results may differ from a plain program's by a relative error of at most 0.0035.
The roundings to bfloat16 on the way count: a program that leaves them out, or rounds other values in their place, can miss the bound.
Values may be sent and summed in bfloat16 or wider, within the bound.
No kernel may reach another device: no remote copies, remote signals or barrier semaphores. Data moves between devices by JAX's collectives and lax.ppermute only.
A program may use at most 128 MiB of HBM per device.

v0:
```python
import jax
import jax.numpy as jnp
from jax import lax
from jax.sharding import PartitionSpec as P

ITERS = 4


def per_device(factors, damping):
    fac_grp = factors.shape[0]
    row_count = factors.shape[1]
    order_full = factors.shape[2]
    rep_count = lax.axis_size("rep")
    fac_rep = fac_grp // rep_count
    blk_rows = row_count * rep_count
    blk_idx = lax.axis_index("blk")
    rep_idx = lax.axis_index("rep")
    row_ids = blk_idx * blk_rows + rep_idx * row_count + lax.iota(jnp.int32, row_count)
    col_ids = lax.iota(jnp.int32, order_full)
    eye_block = (row_ids[:, None] == col_ids[None, :]).astype(jnp.float32)
    damped = factors + damping[:, None, None] * eye_block[None, :, :]
    factor_norms = jnp.sqrt(lax.psum(jnp.sum(damped * damped, axis=(1, 2)), ("rep", "blk")))
    own_rows = lax.all_to_all(damped, "rep", split_axis=0, concat_axis=1, tiled=True)
    own_norms = lax.dynamic_slice_in_dim(factor_norms, rep_idx * fac_rep, fac_rep)
    iterate = (own_rows / own_norms[:, None, None]).astype(jnp.bfloat16)
    iter_rows = blk_idx * blk_rows + lax.iota(jnp.int32, blk_rows)
    eye_rows = (iter_rows[:, None] == col_ids[None, :]).astype(jnp.float32)
    inverse = eye_rows[None, :, :].astype(jnp.bfloat16)
    for sweep_idx in range(ITERS):
        whole_iter, whole_inv = (
            lax.all_gather(iterate, "blk", axis=1, tiled=True),
            lax.all_gather(inverse, "blk", axis=1, tiled=True),
        )
        eye_full = jnp.eye(order_full, dtype=jnp.float32)
        moment_full = jnp.einsum(
            "fik,fkj->fij", whole_inv, whole_iter, preferred_element_type=jnp.float32
        )
        step_full = ((3.0 * eye_full[None, :, :] - moment_full) * 0.5).astype(jnp.bfloat16)
        step_rows = lax.dynamic_slice_in_dim(step_full, blk_idx * blk_rows, blk_rows, 1)
        new_iterate = jnp.einsum(
            "fik,fkj->fij", iterate, step_full, preferred_element_type=jnp.float32
        )
        new_inverse = jnp.einsum(
            "fik,fkj->fij", step_rows, whole_inv, preferred_element_type=jnp.float32
        )
        iterate = new_iterate.astype(jnp.bfloat16)
        inverse = new_inverse.astype(jnp.bfloat16)
    root_block, inv_block = (
        lax.all_to_all(iterate, "rep", split_axis=1, concat_axis=0, tiled=True),
        lax.all_to_all(inverse, "rep", split_axis=1, concat_axis=0, tiled=True),
    )
    root_scale = jnp.sqrt(factor_norms)[:, None, None]
    return (root_block.astype(jnp.float32) * root_scale, inv_block.astype(jnp.float32) / root_scale)


def solution(mesh):
    return jax.shard_map(
        per_device,
        mesh=mesh,
        in_specs=(P("grp", ("blk", "rep"), None), P("grp")),
        out_specs=(P("grp", ("blk", "rep"), None), P("grp", ("blk", "rep"), None)),
        check_vma=False,
    )
```

profile of v0, /device:TPU:0, one launch (start us, length us, event | category | flops | bytes accessed | tf_op | source)
XLA Modules:
  0.0 384.2 jit_solution(16059342983351797581)
XLA Ops:
  7.2 0.1 fusion.21
  7.3 4.3 %multiply_reduce_fusion = (f32[8]{0:T(128)S(1)}, f32[8,80,1280]{2,1,0:T(8,128)}) fusion(f32[8,80,1280]{2,1,0:T(8,128)} %param.2, f32[80,1280]{1,0:T(8,128)S(1)} %fusion.21, f32[8]{0:T(128)} %param.3), kind=kLoop, calls=%fused_computation.20 | loop fusion | flops 3276792 | bytes 6963264 | tf_op jit(solution)/shard_map/reduce_sum | solution.py:22
  11.6 7.3 %all-to-all-start = ((f32[8,80,1280]{2,1,0:T(8,128)}), f32[8,80,1280]{2,1,0:T(8,128)S(1)}, u32[]{:S(2)}, u32[]{:S(2)}) async-start(f32[8,80,1280]{2,1,0:T(8,128)} %get-tuple-element.3), calls=%async_computation | async-start | bytes 6553600 | tf_op jit(solution)/shard_map/all_to_all | solution.py:23
  18.9 0.0 all-gather.15.cloned.1.call-start
  19.0 1.5 convert_convert_fusion
  20.5 0.0 all-gather.15.cloned.1.call-update
  20.5 0.0 all-gather.17.cloned.1.call-start
  20.5 80.0 %psum.7 = f32[8]{0:T(128)S(1)} all-reduce(f32[8]{0:T(128)S(1)} %get-tuple-element.2), channel_id=1, replica_groups=mesh['grp'=2,'rep'=8,'blk'=2] {'rep','blk'}, use_global_device_ids=true, to_apply=%region_1.0 | all-reduce | flops 8 | bytes 64 | tf_op jit(solution)/shard_map/psum | solution.py:22
  100.6 0.6 dynamic_slice.2
  101.2 2.0 divide_convert_fusion
  103.2 0.0 all-gather.17.cloned.1.call-update
  103.2 0.0 all-gather.21.cloned.1.call-start
  103.3 0.0 all-gather.15.cloned.1.call-done
  103.3 20.4 %all-gather.17.cloned.1.call-done = bf16[1,1280,1280]{2,1,0:T(8,128)(2,1)} async-done(((bf16[1,640,1280]{2,1,0:T(8,128)(2,1)}), bf16[1,1280,1280]{2,1,0:T(8,128)(2,1)}) %all-gather.17.cloned.1.call-update) | async-done | bytes 3276816 | tf_op jit(solution)/shard_map/all_gather | solution.py:31
  123.7 7.3 %fusion.4 = bf16[1280,1280]{1,0:T(8,128)(2,1)S(1)} fusion(bf16[1,1280,1280]{2,1,0:T(8,128)(2,1)} %all-gather.17.cloned.1.call-done, bf16[1,1280,1280]{2,1,0:T(8,128)(2,1)} %all-gather.15.cloned.1.call-done), kind=kOutput, calls=%fused_computation.8 | convolution fusion | flops 4202496000 | bytes 9830400 | tf_op jit(solution)/shard_map/fik,fkj->fij/dot_general | solution.py:35
  131.1 1.7 copy-done.5
  132.8 3.5 convolution_convert_fusion.6
  136.3 0.0 all-gather.21.cloned.1.call-update
  136.3 0.0 all-gather.19.cloned.1.call-start
  136.4 5.9 %fusion.12 = bf16[640,1280]{1,0:T(8,128)(2,1)} fusion(bf16[1,1280,1280]{2,1,0:T(8,128)(2,1)} %all-gather.15.cloned.1.call-done, bf16[1280,1280]{1,0:T(8,128)(2,1)} %copy-done.5, s32[]{:T(128)S(6)} %select_n.10), kind=kOutput, calls=%fused_computation.22 | convolution fusion | flops 2097971200 | bytes 6553604 | tf_op jit(solution)/shard_map/fik,fkj->fij/dot_general | solution.py:43
  142.3 0.0 all-gather.19.cloned.1.call-update
  142.3 0.2 all-gather.25.cloned.1.call-start
  142.5 7.5 %all-gather.21.cloned.1.call-done = bf16[1280,1280]{1,0:T(8,128)(2,1)} async-done(((bf16[640,1280]{1,0:T(8,128)(2,1)}), bf16[1280,1280]{1,0:T(8,128)(2,1)}) %all-gather.21.cloned.1.call-update) | async-done | bytes 3276816 | tf_op jit(solution)/shard_map/all_gather | solution.py:31
  150.0 15.5 %all-gather.19.cloned.1.call-done = bf16[1280,1280]{1,0:T(8,128)(2,1)} async-done(((bf16[640,1280]{1,0:T(8,128)(2,1)}), bf16[1280,1280]{1,0:T(8,128)(2,1)}) %all-gather.19.cloned.1.call-update) | async-done | bytes 3276816 | tf_op jit(solution)/shard_map/all_gather | solution.py:32
  165.5 7.3 %fusion.5 = bf16[1280,1280]{1,0:T(8,128)(2,1)S(1)} fusion(bf16[1280,1280]{1,0:T(8,128)(2,1)} %all-gather.19.cloned.1.call-done, bf16[1280,1280]{1,0:T(8,128)(2,1)} %all-gather.21.cloned.1.call-done), kind=kOutput, calls=%fused_computation.9 | convolution fusion | flops 4202496000 | bytes 9830400 | tf_op jit(solution)/shard_map/fik,fkj->fij/dot_general | solution.py:35
  172.8 0.0 copy-start.7
  172.8 1.7 copy-done.7
  174.5 3.5 convolution_convert_fusion.5
  178.0 0.0 all-gather.25.cloned.1.call-update
  178.1 0.0 all-gather.23.cloned.1.call-start
  178.1 5.9 %convolution_convert_fusion.4 = bf16[640,1280]{1,0:T(8,128)(2,1)} fusion(bf16[1280,1280]{1,0:T(8,128)(2,1)} %all-gather.19.cloned.1.call-done, bf16[1280,1280]{1,0:T(8,128)(2,1)} %copy-done.7, s32[]{:T(128)S(6)} %select_n.10), kind=kOutput, calls=%fused_computation.27 | convolution fusion | flops 2097971200 | bytes 6553604 | tf_op jit(solution)/shard_map/fik,fkj->fij/dot_general | solution.py:43
  184.0 0.0 all-gather.23.cloned.1.call-update
  184.0 0.0 all-gather.29.cloned.1.call-start
  184.1 7.6 %all-gather.25.cloned.1.call-done = bf16[1280,1280]{1,0:T(8,128)(2,1)} async-done(((bf16[640,1280]{1,0:T(8,128)(2,1)}), bf16[1280,1280]{1,0:T(8,128)(2,1)}) %all-gather.25.cloned.1.call-update) | async-done | bytes 3276816 | tf_op jit(solution)/shard_map/all_gather | solution.py:31
  191.7 15.5 %all-gather.23.cloned.1.call-done = bf16[1280,1280]{1,0:T(8,128)(2,1)} async-done(((bf16[640,1280]{1,0:T(8,128)(2,1)}), bf16[1280,1280]{1,0:T(8,128)(2,1)}) %all-gather.23.cloned.1.call-update) | async-done | bytes 3276816 | tf_op jit(solution)/shard_map/all_gather | solution.py:32
  207.2 7.3 %fusion.6 = bf16[1280,1280]{1,0:T(8,128)(2,1)S(1)} fusion(bf16[1280,1280]{1,0:T(8,128)(2,1)} %all-gather.23.cloned.1.call-done, bf16[1280,1280]{1,0:T(8,128)(2,1)} %all-gather.25.cloned.1.call-done), kind=kOutput, calls=%fused_computation.10 | convolution fusion | flops 4202496000 | bytes 9830400 | tf_op jit(solution)/shard_map/fik,fkj->fij/dot_general | solution.py:35
  214.5 0.0 copy-start.8
  214.5 1.7 copy-done.8
  216.2 3.5 convolution_convert_fusion.3
  219.8 0.0 all-gather.29.cloned.1.call-update
  219.8 0.3 all-gather.27.cloned.1.call-start
  220.0 5.9 %convolution_convert_fusion.2 = bf16[640,1280]{1,0:T(8,128)(2,1)} fusion(bf16[1280,1280]{1,0:T(8,128)(2,1)} %all-gather.23.cloned.1.call-done, bf16[1280,1280]{1,0:T(8,128)(2,1)} %copy-done.8, s32[]{:T(128)S(6)} %select_n.10), kind=kOutput, calls=%fused_computation.25 | convolution fusion | flops 2097971200 | bytes 6553604 | tf_op jit(solution)/shard_map/fik,fkj->fij/dot_general | solution.py:43
  225.9 0.0 all-gather.27.cloned.1.call-update
  226.0 7.5 %all-gather.29.cloned.1.call-done = bf16[1280,1280]{1,0:T(8,128)(2,1)} async-done(((bf16[640,1280]{1,0:T(8,128)(2,1)}), bf16[1280,1280]{1,0:T(8,128)(2,1)}) %all-gather.29.cloned.1.call-update) | async-done | bytes 3276816 | tf_op jit(solution)/shard_map/all_gather | solution.py:31
  233.4 15.6 %all-gather.27.cloned.1.call-done = bf16[1280,1280]{1,0:T(8,128)(2,1)} async-done(((bf16[640,1280]{1,0:T(8,128)(2,1)}), bf16[1280,1280]{1,0:T(8,128)(2,1)}) %all-gather.27.cloned.1.call-update) | async-done | bytes 3276816 | tf_op jit(solution)/shard_map/all_gather | solution.py:32
  249.1 7.3 %fusion.7 = bf16[1280,1280]{1,0:T(8,128)(2,1)S(1)} fusion(bf16[1280,1280]{1,0:T(8,128)(2,1)} %all-gather.27.cloned.1.call-done, bf16[1280,1280]{1,0:T(8,128)(2,1)} %all-gather.29.cloned.1.call-done), kind=kOutput, calls=%fused_computation.11 | convolution fusion | flops 4202496000 | bytes 9830400 | tf_op jit(solution)/shard_map/fik,fkj->fij/dot_general | solution.py:35
  256.4 2.3 fusion.15
  258.7 2.5 copy.11
  261.3 0.6 broadcast.81
  261.9 12.2 %reduce.1 = bf16[640,1280]{1,0:T(8,128)(2,1)} reduce(bf16[640,1,1280]{2,1,0:T(2,128)(2,1)S(1)} %bitcast.46, bf16[]{:T(256)} %broadcast.81), dimensions={1}, to_apply=%bitcast.43.reduce_sub_computation | reduce | bytes 3276802
  274.1 3.9 %reshape.220 = bf16[8,2,51200]{2,1,0:T(2,128)(2,1)} reshape(bf16[640,1280]{1,0:T(8,128)(2,1)} %reduce.1) | data formatting | bytes 3276800
  278.0 5.9 %all-to-all-start.1 = ((bf16[8,2,51200]{2,1,0:T(2,128)(2,1)}), bf16[8,2,51200]{2,1,0:T(2,128)(2,1)}, u32[]{:S(2)}, u32[]{:S(2)}) async-start(bf16[8,2,51200]{2,1,0:T(2,128)(2,1)} %reshape.220), calls=%async_computation.1 | async-start | bytes 3276800 | tf_op jit(solution)/shard_map/all_to_all | solution.py:49
  284.0 3.7 fusion.16
  287.7 2.5 copy.10
  290.2 12.1 %reduce = bf16[640,1280]{1,0:T(8,128)(2,1)} reduce(bf16[640,1,1280]{2,1,0:T(2,128)(2,1)S(1)} %bitcast.47, bf16[]{:T(256)} %broadcast.81), dimensions={1}, to_apply=%bitcast.42.reduce_sub_computation | reduce | bytes 3276802
  302.3 3.7 reshape.222
  306.0 16.8 %all-to-all-done.1 = bf16[8,2,51200]{2,1,0:T(2,128)(2,1)} async-done(((bf16[8,2,51200]{2,1,0:T(2,128)(2,1)}), bf16[8,2,51200]{2,1,0:T(2,128)(2,1)}, u32[]{:S(2)}, u32[]{:S(2)}) %all-to-all-start.1) | async-done | bytes 1638432 | tf_op jit(solution)/shard_map/all_to_all | solution.py:49
  322.8 4.3 %all-to-all-start.2 = ((bf16[8,2,51200]{2,1,0:T(2,128)(2,1)}), bf16[8,2,51200]{2,1,0:T(2,128)(2,1)}, u32[]{:S(2)}, u32[]{:S(2)}) async-start(bf16[8,2,51200]{2,1,0:T(2,128)(2,1)} %reshape.222), calls=%async_computation.2 | async-start | bytes 3276800 | tf_op jit(solution)/shard_map/all_to_all | solution.py:50
  327.1 6.4 %reshape.221 = bf16[640,1,1280]{2,1,0:T(2,128)(2,1)} reshape(bf16[8,2,51200]{2,1,0:T(2,128)(2,1)} %all-to-all-done.1) | data formatting | bytes 3276800
  333.5 2.1 copy.6
  335.6 29.5 %all-to-all-done.2 = bf16[8,2,51200]{2,1,0:T(2,128)(2,1)} async-done(((bf16[8,2,51200]{2,1,0:T(2,128)(2,1)}), bf16[8,2,51200]{2,1,0:T(2,128)(2,1)}, u32[]{:S(2)}, u32[]{:S(2)}) %all-to-all-start.2) | async-done | bytes 1638432 | tf_op jit(solution)/shard_map/all_to_all | solution.py:50
  365.1 6.4 %reshape.223 = bf16[640,1,1280]{2,1,0:T(2,128)(2,1)} reshape(bf16[8,2,51200]{2,1,0:T(2,128)(2,1)} %all-to-all-done.2) | data formatting | bytes 3276800
  371.5 2.1 copy.7
  373.6 3.5 broadcast_divide_fusion
  (17 shorter events, 0.1 us)
Async XLA Ops:
  11.6 89.6 %all-to-all-start = ((f32[8,80,1280]{2,1,0:T(8,128)}), f32[8,80,1280]{2,1,0:T(8,128)S(1)}, u32[]{:S(2)}, u32[]{:S(2)}) async-start(f32[8,80,1280]{2,1,0:T(8,128)} %get-tuple-element.3), calls=%async_computation | async-start | bytes 6553600 | tf_op jit(solution)/shard_map/all_to_all | solution.py:23
  18.9 84.4 %all-gather.15.cloned.1.call-start = ((), (), s32[]{:S(2)}) async-start(), calls=%async_computation.3 | async-start | bytes 4915200 | tf_op jit(solution)/shard_map/all_gather | solution.py:32
  20.5 103.3 %all-gather.17.cloned.1.call-start = ((), (), s32[]{:S(2)}) async-start(), calls=%async_computation.4 | async-start | bytes 4915200 | tf_op jit(solution)/shard_map/all_gather | solution.py:31
  103.2 29.6 %copy-start = (bf16[8,80,1280]{2,1,0:T(8,128)(2,1)S(1)}, bf16[8,80,1280]{2,1,0:T(8,128)(2,1)}, u32[]{:S(2)}) copy-start(bf16[8,80,1280]{2,1,0:T(8,128)(2,1)} %divide_convert_fusion) | copy-start | bytes 4915204
  103.2 46.7 %all-gather.21.cloned.1.call-start = ((), (), s32[]{:S(2)}) async-start(), calls=%async_computation.6 | async-start | bytes 4915200 | tf_op jit(solution)/shard_map/all_gather | solution.py:31
  131.1 1.7 copy-start.5
  136.3 29.1 %all-gather.19.cloned.1.call-start = ((), (), s32[]{:S(2)}) async-start(), calls=%async_computation.5 | async-start | bytes 4915200 | tf_op jit(solution)/shard_map/all_gather | solution.py:32
  142.3 32.2 %copy-start.1 = (bf16[640,1280]{1,0:T(8,128)(2,1)S(1)}, bf16[640,1280]{1,0:T(8,128)(2,1)}, u32[]{:S(2)}) copy-start(bf16[640,1280]{1,0:T(8,128)(2,1)} %convolution_convert_fusion.6) | copy-start | bytes 4915204
  142.3 49.4 %all-gather.25.cloned.1.call-start = ((), (), s32[]{:S(2)}) async-start(), calls=%async_computation.8 | async-start | bytes 4915200 | tf_op jit(solution)/shard_map/all_gather | solution.py:31
  172.8 1.7 copy-start.7
  178.1 29.1 %all-gather.23.cloned.1.call-start = ((), (), s32[]{:S(2)}) async-start(), calls=%async_computation.7 | async-start | bytes 4915200 | tf_op jit(solution)/shard_map/all_gather | solution.py:32
  184.0 32.2 %copy-start.2 = (bf16[640,1280]{1,0:T(8,128)(2,1)S(1)}, bf16[640,1280]{1,0:T(8,128)(2,1)}, u32[]{:S(2)}) copy-start(bf16[640,1280]{1,0:T(8,128)(2,1)} %convolution_convert_fusion.5) | copy-start | bytes 4915204
  184.0 49.4 %all-gather.29.cloned.1.call-start = ((), (), s32[]{:S(2)}) async-start(), calls=%async_computation.10 | async-start | bytes 4915200 | tf_op jit(solution)/shard_map/all_gather | solution.py:31
  214.5 1.7 copy-start.8
  219.8 29.3 %all-gather.27.cloned.1.call-start = ((), (), s32[]{:S(2)}) async-start(), calls=%async_computation.9 | async-start | bytes 4915200 | tf_op jit(solution)/shard_map/all_gather | solution.py:32
  225.9 30.5 %copy-start.3 = (bf16[640,1280]{1,0:T(8,128)(2,1)S(1)}, bf16[640,1280]{1,0:T(8,128)(2,1)}, u32[]{:S(2)}) copy-start(bf16[640,1280]{1,0:T(8,128)(2,1)} %convolution_convert_fusion.3) | copy-start | bytes 4915204
  256.4 2.3 copy-start.6
  274.1 9.9 %copy-start.4 = (bf16[1280,1280]{1,0:T(8,128)(2,1)S(1)}, bf16[1280,1280]{1,0:T(8,128)(2,1)}, u32[]{:S(2)}) copy-start(bf16[1280,1280]{1,0:T(8,128)(2,1)} %all-gather.27.cloned.1.call-done) | copy-start | bytes 9830404
  278.0 44.8 %all-to-all-start.1 = ((bf16[8,2,51200]{2,1,0:T(2,128)(2,1)}), bf16[8,2,51200]{2,1,0:T(2,128)(2,1)}, u32[]{:S(2)}, u32[]{:S(2)}) async-start(bf16[8,2,51200]{2,1,0:T(2,128)(2,1)} %reshape.220), calls=%async_computation.1 | async-start | bytes 3276800 | tf_op jit(solution)/shard_map/all_to_all | solution.py:49
  322.8 42.3 %all-to-all-start.2 = ((bf16[8,2,51200]{2,1,0:T(2,128)(2,1)}), bf16[8,2,51200]{2,1,0:T(2,128)(2,1)}, u32[]{:S(2)}, u32[]{:S(2)}) async-start(bf16[8,2,51200]{2,1,0:T(2,128)(2,1)} %reshape.222), calls=%async_computation.2 | async-start | bytes 3276800 | tf_op jit(solution)/shard_map/all_to_all | solution.py:50
Sparse Core Ops, SparseCore 0:
  21.8 13.7 all-gather.14
  103.3 20.3 all-gather.16
  136.4 13.4 all-gather.20
  151.9 13.4 all-gather.18
  178.2 13.4 all-gather.24
  193.7 13.4 all-gather.22
  219.9 13.4 all-gather.28
  235.5 13.4 all-gather.26
where the time goes:
time: 391 us; the launch traced here: 384 us
  waiting for transfers between devices  136 us (35%)
  blocking collectives  80 us (20%)
  matrix products  63.5 us (16%)
  local copies, waits for them, and re-layouts  36.1 us (9%)
  other arithmetic  35.8 us (9%)
  starting transfers between devices  18.3 us (5%)
  between operations  14.6 us (4%)
    psum x1, blocking collectives, per_device(): lax.psum(jnp.sum(damped * damped, axis=(1, 2)), ('rep', 'blk'))  80 us
    all_gather x4, waiting for transfers between devices, per_device(): lax.all_gather(inverse, 'blk', axis=1, tiled=True)  46.7 us
    all_gather x4, waiting for transfers between devices, per_device(): lax.all_gather(iterate, 'blk', axis=1, tiled=True)  43 us
    unnamed x25, local copies, waits for them, and re-layouts  30.4 us
    all_to_all x1, waiting for transfers between devices, per_device(): lax.all_to_all(inverse, 'rep', split_axis=1, concat_axis=0, tiled=True)  29.5 us
    dot_general x4, matrix products, per_device(): jnp.einsum('fik,fkj->fij', whole_inv, whole_iter, preferred_element_type=...  29.3 us
    unnamed x2, other arithmetic  24.3 us
    dot_general x4, matrix products, per_device(): jnp.einsum('fik,fkj->fij', step_rows, whole_inv, preferred_element_type=j...  21.3 us
  transfers between devices with their start and end apart: 11, of which 9 were waited for; matrix products, arithmetic and copies ran while one was open for 14% of the time, Pallas kernels for 0%

commit v1 on v0

v1 whole, which is shorter than its diff:
```python
import jax
import jax.numpy as jnp
from jax import lax
from jax.sharding import PartitionSpec as P

ITERS = 4


def per_device(factors, damping):
    fac_grp, row_count, order_full = factors.shape
    rep_count = lax.axis_size("rep")
    fac_rep = fac_grp // rep_count
    blk_rows = row_count * rep_count
    blk_idx = lax.axis_index("blk")
    rep_idx = lax.axis_index("rep")
    col_ids = lax.iota(jnp.int32, order_full)
    row_ids = blk_idx * blk_rows + rep_idx * row_count + lax.iota(jnp.int32, row_count)
    eye_block = (row_ids[:, None] == col_ids[None, :]).astype(jnp.float32)
    damped = factors + damping[:, None, None] * eye_block[None, :, :]
    factor_norms = jnp.sqrt(lax.psum(jnp.sum(damped * damped, axis=(1, 2)), ("rep", "blk")))
    scaled = (damped / factor_norms[:, None, None]).astype(jnp.bfloat16)
    scaled = scaled.reshape(rep_count, fac_rep, row_count, order_full)
    own = lax.all_to_all(scaled, "rep", split_axis=0, concat_axis=0, tiled=True)
    iterate = jnp.swapaxes(own, 0, 1).reshape(fac_rep, blk_rows, order_full)

    iter_rows = blk_idx * blk_rows + lax.iota(jnp.int32, blk_rows)
    eye_rows = (iter_rows[:, None] == col_ids[None, :]).astype(jnp.float32)[None]
    swap = ((0, 1), (1, 0))

    def own_cols(mat):
        return lax.dynamic_slice_in_dim(mat, blk_idx * blk_rows, blk_rows, 2)

    def peer_cols(mat):
        return lax.dynamic_slice_in_dim(mat, (1 - blk_idx) * blk_rows, blk_rows, 2)

    def rows_times(left, right_rows):
        peer_rows = lax.ppermute(right_rows, "blk", swap)
        first = jnp.einsum(
            "fik,fkj->fij", own_cols(left), right_rows, preferred_element_type=jnp.float32
        )
        second = jnp.einsum(
            "fik,fkj->fij", peer_cols(left), peer_rows, preferred_element_type=jnp.float32
        )
        return first + second

    step_rows = ((3.0 * eye_rows - iterate.astype(jnp.float32)) * 0.5).astype(jnp.bfloat16)
    iterate = rows_times(iterate, step_rows).astype(jnp.bfloat16)
    inverse = step_rows
    for sweep_idx in range(1, ITERS):
        moment = rows_times(inverse, iterate)
        step_rows = ((3.0 * eye_rows - moment) * 0.5).astype(jnp.bfloat16)
        both = jnp.concatenate([iterate, inverse], axis=1)
        both = rows_times(both, step_rows).astype(jnp.bfloat16)
        iterate, inverse = both[:, :blk_rows], both[:, blk_rows:]

    def send_back(mat):
        blocks = mat.reshape(fac_rep, rep_count, row_count, order_full)
        blocks = jnp.swapaxes(blocks, 0, 1)
        back = lax.all_to_all(blocks, "rep", split_axis=0, concat_axis=0, tiled=True)
        return back.reshape(fac_grp, row_count, order_full).astype(jnp.float32)

    root_scale = jnp.sqrt(factor_norms)[:, None, None]
    return (send_back(iterate) * root_scale, send_back(inverse) / root_scale)


def solution(mesh):
    return jax.shard_map(
        per_device,
        mesh=mesh,
        in_specs=(P("grp", ("blk", "rep"), None), P("grp")),
        out_specs=(P("grp", ("blk", "rep"), None), P("grp", ("blk", "rep"), None)),
        check_vma=False,
    )
```

time: 391 us -> 214 us (0.55); the launches traced: 384 us -> 214 us
  waiting for transfers between devices: 136 us -> 46.1 us
  blocking collectives: 80 us -> 119 us
  local copies, waits for them, and re-layouts: 36.1 us -> 1.41 us
  matrix products: 63.5 us -> 32 us
  other arithmetic: 35.8 us -> 9.91 us
  between operations: 14.6 us -> 0.85 us
  starting transfers between devices: 18.3 us -> 4.79 us
    all_gather x8 -> x0, waiting for transfers between devices: 89.6 us -> none  [the longest x4 46.7 us: per_device(): lax.all_gather(inverse, 'blk', axis=1, tiled=True)]
    all_to_all x0 -> x2, blocking collectives: none -> 84.2 us  [send_back(): lax.all_to_all(blocks, 'rep', split_axis=0, concat_axis=0, tiled=True)]
    psum x1, blocking collectives: 80 us -> 34.9 us  [per_device(): lax.psum(jnp.sum(damped * damped, axis=(1, 2)), ('rep', 'blk'))]
    dot_general x12 -> x14, matrix products: 63.5 us -> 32 us  [the longest x7 17.9 us: rows_times(): jnp.einsum('fik,fkj->fij', peer_cols(left), peer_rows, preferred_element_...]
    unnamed x25 -> x6, local copies, waits for them, and re-layouts: 30.4 us -> 0.76 us
    unnamed x2 -> x0, other arithmetic: 24.3 us -> none
    all_to_all x3 -> x1, starting transfers between devices: 17.5 us -> 3.58 us  [per_device(): own = lax.all_to_all(scaled, 'rep', split_axis=0, concat_axis=0, tiled=True)]
    all_to_all x3 -> x1, waiting for transfers between devices: 46.3 us -> 36.3 us  [per_device(): own = lax.all_to_all(scaled, 'rep', split_axis=0, concat_axis=0, tiled=True)]
  transfers between devices with their start and end apart: 11 -> 8, of which waited for: 9 -> 8; matrix products, arithmetic and copies ran while one was open for 14% -> 7% of each run, Pallas kernels for 0% -> 0%
where the time goes in v1:
time: 214 us
  blocking collectives  119 us (56%)
  waiting for transfers between devices  46.1 us (22%)
  matrix products  32 us (15%)
  other arithmetic  9.91 us (5%)
  starting transfers between devices  4.79 us (2%)
    all_to_all x2, blocking collectives, send_back(): lax.all_to_all(blocks, 'rep', split_axis=0, concat_axis=0, tiled=True)  84.2 us
    all_to_all x1, waiting for transfers between devices, per_device(): own = lax.all_to_all(scaled, 'rep', split_axis=0, concat_axis=0, tiled=True)  36.3 us
    psum x1, blocking collectives, per_device(): lax.psum(jnp.sum(damped * damped, axis=(1, 2)), ('rep', 'blk'))  34.9 us
    dot_general x7, matrix products, rows_times(): jnp.einsum('fik,fkj->fij', peer_cols(left), peer_rows, preferred_element_...  17.9 us
    dot_general x7, matrix products, rows_times(): jnp.einsum('fik,fkj->fij', own_cols(left), right_rows, preferred_element_...  14.1 us
    ppermute x7, waiting for transfers between devices, rows_times(): peer_rows = lax.ppermute(right_rows, 'blk', swap)  9.73 us
  transfers between devices with their start and end apart: 8, of which 8 were waited for; matrix products, arithmetic and copies ran while one was open for 7% of the time, Pallas kernels for 0%

profile of v1, /device:TPU:0, one launch (start us, length us, event | category | flops | bytes accessed | tf_op | source)
XLA Modules:
  0.0 214.1 jit_solution(8542991458444012617)
XLA Ops:
  0.6 0.0 copy-start.2
  0.6 0.0 copy-start
  0.7 0.1 fusion.62
  0.8 0.0 copy-start.1
  0.8 0.7 copy-done.1
  1.5 2.8 %multiply_reduce_fusion = f32[8]{0:T(128)S(1)} fusion(f32[8,80,1280]{2,1,0:T(8,128)} %param.2, f32[80,1280]{1,0:T(8,128)S(1)} %fusion.62, f32[8]{0:T(128)} %param.3), kind=kLoop, calls=%fused_computation.31 | loop fusion | flops 3276792 | bytes 3686464 | tf_op jit(solution)/shard_map/reduce_sum | solution.py:20
  4.4 34.9 %psum.7 = f32[8]{0:T(128)S(1)} all-reduce(f32[8]{0:T(128)S(1)} %multiply_reduce_fusion), channel_id=1, replica_groups=mesh['grp'=2,'rep'=8,'blk'=2] {'rep','blk'}, use_global_device_ids=true, to_apply=%region_1.0 | all-reduce | flops 8 | bytes 64 | tf_op jit(solution)/shard_map/psum | solution.py:20
  39.3 0.0 copy-done.2
  39.3 0.0 copy-done
  39.3 2.7 %fusion.44 = bf16[8,1,80,1280]{3,2,1,0:T(8,128)(2,1)} fusion(f32[8]{0:T(128)S(1)} %get-tuple-element.11, f32[8,80,1280]{2,1,0:T(8,128)S(1)} %copy-done, f32[80,1280]{1,0:T(8,128)} %copy-done.1, f32[8]{0:T(128)S(1)} %copy-done.2), kind=kLoop, calls=%fused_computation.65 | loop fusion | flops 3276800 | bytes 5324864 | tf_op jit(solution)/shard_map/reshape | solution.py:22
  42.0 3.6 %all-to-all-start = ((bf16[8,1,80,1280]{3,2,1,0:T(8,128)(2,1)}), bf16[8,1,80,1280]{3,2,1,0:T(8,128)(2,1)S(1)}, u32[]{:S(2)}, u32[]{:S(2)}) async-start(bf16[8,1,80,1280]{3,2,1,0:T(8,128)(2,1)} %fusion.44), calls=%async_computation | async-start | bytes 3276800 | tf_op jit(solution)/shard_map/all_to_all | solution.py:23
  45.6 36.3 %all-to-all-done = bf16[8,1,80,1280]{3,2,1,0:T(8,128)(2,1)S(1)} async-done(((bf16[8,1,80,1280]{3,2,1,0:T(8,128)(2,1)}), bf16[8,1,80,1280]{3,2,1,0:T(8,128)(2,1)S(1)}, u32[]{:S(2)}, u32[]{:S(2)}) %all-to-all-start) | async-done | bytes 1638432 | tf_op jit(solution)/shard_map/all_to_all | solution.py:23
  81.9 0.7 multiply_convert_fusion
  82.7 0.1 collective-permute-start
  82.8 1.6 fusion.14
  84.4 2.0 collective-permute-done
  86.4 2.9 %fusion.12 = bf16[640,1280]{1,0:T(8,128)(2,1)S(1)} fusion(f32[640,1280]{1,0:T(8,128)S(1)} %fusion.14, bf16[1,640,1280]{2,1,0:T(8,128)(2,1)} %collective-permute-done, bf16[1,640,1280]{2,1,0:T(8,128)(2,1)S(1)} %bitcast.94, s32[]{:T(128)S(6)} %select_n.5), kind=kOutput, calls=%fused_computation.36 | convolution fusion | flops 1050214400 | bytes 7372804 | tf_op jit(solution)/shard_map/fik,fkj->fij/dot_general | solution.py:41
  89.3 0.2 collective-permute-start.1
  89.5 1.4 fusion.50
  91.0 1.9 collective-permute-done.1
  92.9 1.6 fusion.11
  94.5 0.2 collective-permute-start.2
  94.7 2.7 %fusion.21 = f32[1280,1280]{1,0:T(8,128)S(1)} fusion(bf16[640,1280]{1,0:T(8,128)(2,1)S(1)} %fusion.11, s32[]{:T(128)S(6)} %select_n.4, bf16[1,640,1280]{2,1,0:T(8,128)(2,1)S(1)} %bitcast.102, bf16[1,640,1280]{2,1,0:T(8,128)(2,1)S(1)} %multiply_convert_fusion), kind=kOutput, calls=%fused_computation.43 | convolution fusion | flops 2100428800 | bytes 11468804 | tf_op jit(solution)/shard_map/fik,fkj->fij/dot_general | solution.py:38
  97.5 0.6 collective-permute-done.2
  98.1 4.1 %fusion = bf16[1280,1280]{1,0:T(8,128)(2,1)S(1)} fusion(f32[1280,1280]{1,0:T(8,128)S(1)} %fusion.21, s32[]{:T(128)S(6)} %select_n.5, bf16[1,640,1280]{2,1,0:T(8,128)(2,1)S(1)} %bitcast.103, bf16[1,640,1280]{2,1,0:T(8,128)(2,1)S(1)} %multiply_convert_fusion, bf16[1,640,1280]{2,1,0:T(8,128)(2,1)S(1)} %collective-permute-done.2), kind=kOutput, calls=%fused_computation.3 | convolution fusion | flops 2103705600 | bytes 14745604 | tf_op jit(solution)/shard_map/fik,fkj->fij/dot_general | solution.py:41
  102.2 0.2 fusion.86
  102.4 0.2 collective-permute-start.3
  102.6 1.4 fusion.29
  104.1 1.9 collective-permute-done.3
  106.0 1.6 fusion.10
  107.6 0.2 collective-permute-start.4
  107.8 2.7 %fusion.38 = f32[1280,1280]{1,0:T(8,128)S(1)} fusion(bf16[640,1280]{1,0:T(8,128)(2,1)S(1)} %fusion.10, bf16[1280,1280]{1,0:T(8,128)(2,1)S(1)} %fusion, s32[]{:T(128)S(6)} %select_n.4), kind=kOutput, calls=%fused_computation.59 | convolution fusion | flops 2097152000 | bytes 9830404 | tf_op jit(solution)/shard_map/fik,fkj->fij/dot_general | solution.py:38
  110.5 0.7 collective-permute-done.4
  111.2 3.0 %fusion.1 = bf16[1280,1280]{1,0:T(8,128)(2,1)S(1)} fusion(f32[1280,1280]{1,0:T(8,128)S(1)} %fusion.38, bf16[1,640,1280]{2,1,0:T(8,128)(2,1)S(1)} %collective-permute-done.4, bf16[1280,1280]{1,0:T(8,128)(2,1)S(1)} %fusion, s32[]{:T(128)S(6)} %select_n.5), kind=kOutput, calls=%fused_computation.4 | convolution fusion | flops 2100428800 | bytes 13107204 | tf_op jit(solution)/shard_map/fik,fkj->fij/dot_general | solution.py:41
  114.2 0.2 fusion.85
  114.4 0.1 collective-permute-start.5
  114.5 1.4 fusion.25
  116.0 2.0 collective-permute-done.5
  118.0 1.6 fusion.9
  119.6 0.2 collective-permute-start.6
  119.8 2.7 %fusion.35 = f32[1280,1280]{1,0:T(8,128)S(1)} fusion(bf16[640,1280]{1,0:T(8,128)(2,1)S(1)} %fusion.9, bf16[1280,1280]{1,0:T(8,128)(2,1)S(1)} %fusion.1, s32[]{:T(128)S(6)} %select_n.4), kind=kOutput, calls=%fused_computation.56 | convolution fusion | flops 2097152000 | bytes 9830404 | tf_op jit(solution)/shard_map/fik,fkj->fij/dot_general | solution.py:38
  122.5 0.6 collective-permute-done.6
  123.2 3.0 %fusion.3 = bf16[1,1280,1280]{2,1,0:T(8,128)(2,1)S(1)} fusion(f32[1280,1280]{1,0:T(8,128)S(1)} %fusion.35, bf16[1,640,1280]{2,1,0:T(8,128)(2,1)S(1)} %collective-permute-done.6, bf16[1280,1280]{1,0:T(8,128)(2,1)S(1)} %fusion.1, s32[]{:T(128)S(6)} %select_n.5), kind=kOutput, calls=%fused_computation.6 | convolution fusion | flops 2100428800 | bytes 13107204 | tf_op jit(solution)/shard_map/fik,fkj->fij/dot_general | solution.py:41
  126.2 0.2 fusion.84
  126.4 42.4 %all_to_all.15 = bf16[8,1,80,1280]{3,2,1,0:T(8,128)(2,1)S(1)} all-to-all(bf16[8,1,80,1280]{3,2,1,0:T(8,128)(2,1)S(1)} %bitcast.96), channel_id=1, replica_groups=mesh['grp'=2,'rep'=8,'blk'=2] {'rep'}, dimensions={0} | all-to-all | bytes 3276800 | tf_op jit(solution)/shard_map/all_to_all | solution.py:59
  168.8 41.8 %all_to_all.16 = bf16[8,1,80,1280]{3,2,1,0:T(8,128)(2,1)S(1)} all-to-all(bf16[8,1,80,1280]{3,2,1,0:T(8,128)(2,1)S(1)} %bitcast.95), channel_id=1, replica_groups=mesh['grp'=2,'rep'=8,'blk'=2] {'rep'}, dimensions={0} | all-to-all | bytes 3276800 | tf_op jit(solution)/shard_map/all_to_all | solution.py:59
  210.6 3.5 %convert_divide_fusion = (f32[8,80,1280]{2,1,0:T(8,128)}, f32[8,80,1280]{2,1,0:T(8,128)}) fusion(bf16[8,1,80,1280]{3,2,1,0:T(8,128)(2,1)S(1)} %all_to_all.16, f32[8]{0:T(128)S(1)} %get-tuple-element.10, bf16[8,1,80,1280]{3,2,1,0:T(8,128)(2,1)S(1)} %all_to_all.15), kind=kLoop, calls=%fused_computation.21 | loop fusion | flops 3276800 | bytes 9830432 | tf_op jit(solution)/shard_map/div | solution.py:63
  (3 shorter events, 0.0 us)
Async XLA Ops:
  0.6 38.7 %copy-start.2 = (f32[8]{0:T(128)S(1)}, f32[8]{0:T(128)}, u32[]{:S(2)}) copy-start(f32[8]{0:T(128)} %param.3) | copy-start | bytes 100
  0.6 38.7 %copy-start = (f32[8,80,1280]{2,1,0:T(8,128)S(1)}, f32[8,80,1280]{2,1,0:T(8,128)}, u32[]{:S(2)}) copy-start(f32[8,80,1280]{2,1,0:T(8,128)} %param.2) | copy-start | bytes 9830404
  0.8 0.8 copy-start.1
  42.0 39.9 %all-to-all-start = ((bf16[8,1,80,1280]{3,2,1,0:T(8,128)(2,1)}), bf16[8,1,80,1280]{3,2,1,0:T(8,128)(2,1)S(1)}, u32[]{:S(2)}, u32[]{:S(2)}) async-start(bf16[8,1,80,1280]{3,2,1,0:T(8,128)(2,1)} %fusion.44), calls=%async_computation | async-start | bytes 3276800 | tf_op jit(solution)/shard_map/all_to_all | solution.py:23
  82.7 3.7 %collective-permute-start = (bf16[1,640,1280]{2,1,0:T(8,128)(2,1)S(1)}, bf16[1,640,1280]{2,1,0:T(8,128)(2,1)}, u32[]{:S(2)}, u32[]{:S(2)}) collective-permute-start(bf16[1,640,1280]{2,1,0:T(8,128)(2,1)S(1)} %multiply_convert_fusion), channel_id=1, source_target_pairs={{0,1},{1,0},{2,3},{3,2},{4,5},{5,4},{6,7},{7,6},{8,9},{9,8},{10,11... | collective-permute-start | bytes 4915208 | tf_op jit(solution)/shard_map/ppermute | solution.py:37
  89.3 3.6 %collective-permute-start.1 = (bf16[1,640,1280]{2,1,0:T(8,128)(2,1)S(1)}, bf16[1,640,1280]{2,1,0:T(8,128)(2,1)S(1)}, u32[]{:S(2)}, u32[]{:S(2)}) collective-permute-start(bf16[1,640,1280]{2,1,0:T(8,128)(2,1)S(1)} %bitcast.101), channel_id=1, source_target_pairs={{0,1},{1,0},{2,3},{3,2},{4,5},{5,4},{6,7},{7,6},{8,9},{9,8},{10,11... | collective-permute-start | bytes 4915208 | tf_op jit(solution)/shard_map/ppermute | solution.py:37
  94.5 3.6 %collective-permute-start.2 = (bf16[1,640,1280]{2,1,0:T(8,128)(2,1)S(1)}, bf16[1,640,1280]{2,1,0:T(8,128)(2,1)S(1)}, u32[]{:S(2)}, u32[]{:S(2)}) collective-permute-start(bf16[1,640,1280]{2,1,0:T(8,128)(2,1)S(1)} %bitcast.106), channel_id=1, source_target_pairs={{0,1},{1,0},{2,3},{3,2},{4,5},{5,4},{6,7},{7,6},{8,9},{9,8},{10,11... | collective-permute-start | bytes 4915208 | tf_op jit(solution)/shard_map/ppermute | solution.py:37
  102.4 3.6 %collective-permute-start.3 = (bf16[1,640,1280]{2,1,0:T(8,128)(2,1)S(1)}, bf16[1,640,1280]{2,1,0:T(8,128)(2,1)S(1)}, u32[]{:S(2)}, u32[]{:S(2)}) collective-permute-start(bf16[1,640,1280]{2,1,0:T(8,128)(2,1)S(1)} %get-tuple-element.6), channel_id=1, source_target_pairs={{0,1},{1,0},{2,3},{3,2},{4,5},{5,4},{6,7},{7,6},{8,9},{9,8},{10,11... | collective-permute-start | bytes 4915208 | tf_op jit(solution)/shard_map/ppermute | solution.py:37
  107.6 3.6 %collective-permute-start.4 = (bf16[1,640,1280]{2,1,0:T(8,128)(2,1)S(1)}, bf16[1,640,1280]{2,1,0:T(8,128)(2,1)S(1)}, u32[]{:S(2)}, u32[]{:S(2)}) collective-permute-start(bf16[1,640,1280]{2,1,0:T(8,128)(2,1)S(1)} %bitcast.105), channel_id=1, source_target_pairs={{0,1},{1,0},{2,3},{3,2},{4,5},{5,4},{6,7},{7,6},{8,9},{9,8},{10,11... | collective-permute-start | bytes 4915208 | tf_op jit(solution)/shard_map/ppermute | solution.py:37
  114.4 3.6 %collective-permute-start.5 = (bf16[1,640,1280]{2,1,0:T(8,128)(2,1)S(1)}, bf16[1,640,1280]{2,1,0:T(8,128)(2,1)S(1)}, u32[]{:S(2)}, u32[]{:S(2)}) collective-permute-start(bf16[1,640,1280]{2,1,0:T(8,128)(2,1)S(1)} %get-tuple-element.4), channel_id=1, source_target_pairs={{0,1},{1,0},{2,3},{3,2},{4,5},{5,4},{6,7},{7,6},{8,9},{9,8},{10,11... | collective-permute-start | bytes 4915208 | tf_op jit(solution)/shard_map/ppermute | solution.py:37
  119.6 3.6 %collective-permute-start.6 = (bf16[1,640,1280]{2,1,0:T(8,128)(2,1)S(1)}, bf16[1,640,1280]{2,1,0:T(8,128)(2,1)S(1)}, u32[]{:S(2)}, u32[]{:S(2)}) collective-permute-start(bf16[1,640,1280]{2,1,0:T(8,128)(2,1)S(1)} %bitcast.104), channel_id=1, source_target_pairs={{0,1},{1,0},{2,3},{3,2},{4,5},{5,4},{6,7},{7,6},{8,9},{9,8},{10,11... | collective-permute-start | bytes 4915208 | tf_op jit(solution)/shard_map/ppermute | solution.py:37
